TPU v7x, 32 devices: a whole 2x2x4 slice. The times are simulated.
32 devices in a mesh: cx: 4 (over z), cy: 2 (over y), tp: 4 (over x, core).
Axes of the slice: x: 2, y: 2, z: 4, core: 2. Of those that a mesh axis runs over, the one named last changes fastest.
Arguments:
- neighbor_ids: int32 [16, 8, 128], P(('cx', 'cy'), 'tp'), may hold values from 0 to 1023
- decoder: bfloat16 [16, 64, 896], P(('cx', 'cy')), may hold values from -6 to 6
- table: bfloat16 [1024, 896], P(('cx', 'cy')), may hold values from -6 to 6
- attn_in: bfloat16 [6, 896, 896], P(None, ('cx', 'cy'), 'tp'), may hold values from -0.1875 to 0.1875
- attn_out: bfloat16 [2, 896, 896], P(None, 'tp', ('cx', 'cy')), may hold values from -0.1875 to 0.1875
- gains: float32 [3, 896], replicated, may hold values from 0.25 to 1.75
- w_up: bfloat16 [896, 3584], P(('cx', 'cy'), 'tp'), may hold values from -0.1875 to 0.1875
- w_down: bfloat16 [3584, 896], P('tp', ('cx', 'cy')), may hold values from -0.09375 to 0.09375
Outputs:
- encoded: bfloat16 [16, 8, 128, 896], P(('cx', 'cy'), 'tp')
All inputs are finite; a program needn't handle non-finite values.
Results may differ from a plain program's by a relative error of at most 0.013.
Values may be sent and summed in bfloat16 or wider, within the bound.
No kernel may reach another device: no remote copies, remote signals or barrier semaphores. Data moves between devices by JAX's collectives and lax.ppermute only.
A program may use at most 128 MiB of HBM per device.

v0:
```python
import jax
import jax.numpy as jnp
from jax import lax
from jax.sharding import PartitionSpec as P

HD = 64


def layer_norm(values, gain):
    middle = jnp.mean(values, axis=-1, keepdims=True)
    centred = values - middle
    spread = jnp.mean(centred * centred, axis=-1, keepdims=True)
    return (centred * lax.rsqrt(spread + 1e-05) * gain).astype(jnp.bfloat16)


def project(hidden, matrix):
    return jnp.dot(hidden, matrix, preferred_element_type=jnp.float32).astype(jnp.bfloat16)


def attend(query, key_rows, value_rows):
    batch, q_len, width = query.shape
    k_len = key_rows.shape[1]
    heads = width // HD
    q_heads = query.reshape(batch, q_len, heads, HD)
    k_heads = key_rows.reshape(batch, k_len, heads, HD)
    v_heads = value_rows.reshape(batch, k_len, heads, HD)
    scores = jnp.einsum(
        "bqhd,bkhd->bhqk", q_heads, k_heads, preferred_element_type=jnp.float32
    ) * HD ** (-0.5)
    probs = jax.nn.softmax(scores, axis=-1).astype(jnp.bfloat16)
    mixed = jnp.einsum("bhqk,bkhd->bqhd", probs, v_heads, preferred_element_type=jnp.float32)
    return mixed.reshape(batch, q_len, width).astype(jnp.bfloat16)


def body(neighbor_ids, decoder, table, attn_in, attn_out, gains, w_up, w_down):
    full_table, in_w, out_w, up_w, down_w = (
        lax.all_gather(table, ("cx", "cy"), axis=0, tiled=True),
        lax.all_gather(attn_in, ("cx", "cy"), axis=1, tiled=True),
        lax.all_gather(attn_out, ("cx", "cy"), axis=2, tiled=True),
        lax.all_gather(w_up, ("cx", "cy"), axis=0, tiled=True),
        lax.all_gather(w_down, ("cx", "cy"), axis=1, tiled=True),
    )
    spans, nbrs, length = neighbor_ids.shape
    width = full_table.shape[1]
    dec_len = decoder.shape[1]
    total = spans * nbrs * length
    dec_rows = decoder.reshape(spans * dec_len, width)
    x_zero = jnp.take(full_table, neighbor_ids.reshape(-1), axis=0).astype(jnp.float32)
    h_one = layer_norm(x_zero, gains[0])
    in_full, out_full = (
        lax.all_gather(in_w, "tp", axis=2, tiled=True),
        lax.all_gather(out_w, "tp", axis=1, tiled=True),
    )
    query = project(h_one, in_full[0]).reshape(spans * nbrs, length, width)
    keys = project(h_one, in_full[1]).reshape(spans * nbrs, length, width)
    values = project(h_one, in_full[2]).reshape(spans * nbrs, length, width)
    self_out = attend(query, keys, values).reshape(total, width)
    x_one = x_zero + jnp.dot(self_out, out_full[0], preferred_element_type=jnp.float32)
    h_two = layer_norm(x_one, gains[1])
    cross_q = project(h_two, in_full[3]).reshape(spans, nbrs * length, width)
    cross_k = project(dec_rows, in_full[4]).reshape(spans, dec_len, width)
    cross_v = project(dec_rows, in_full[5]).reshape(spans, dec_len, width)
    cross = attend(cross_q, cross_k, cross_v).reshape(total, width)
    x_two = x_one + jnp.dot(cross, out_full[1], preferred_element_type=jnp.float32)
    h_three = layer_norm(x_two, gains[2])
    every = lax.all_gather(h_three, "tp", axis=0, tiled=True)
    upward = jnp.dot(every, up_w, preferred_element_type=jnp.float32)
    act = jax.nn.gelu(upward, approximate=True).astype(jnp.bfloat16)
    mixed = lax.psum_scatter(
        jnp.dot(act, down_w, preferred_element_type=jnp.float32).astype(jnp.bfloat16),
        "tp",
        scatter_dimension=0,
        tiled=True,
    ).astype(jnp.float32)
    return (x_two + mixed).astype(jnp.bfloat16).reshape(spans, nbrs, length, width)


def solution(mesh):
    in_specs = (
        P(("cx", "cy"), "tp", None),
        P(("cx", "cy"), None, None),
        P(("cx", "cy"), None),
        P(None, ("cx", "cy"), "tp"),
        P(None, "tp", ("cx", "cy")),
        P(),
        P(("cx", "cy"), "tp"),
        P("tp", ("cx", "cy")),
    )
    out_specs = P(("cx", "cy"), "tp", None, None)
    return jax.shard_map(body, mesh=mesh, in_specs=in_specs, out_specs=out_specs, check_vma=False)
```

profile of v0, /device:TPU:0, one launch (start us, length us, event | category | flops | bytes accessed | tf_op | source)
XLA Modules:
  0.0 414.2 jit_solution(9565664598188071752)
XLA Ops:
  9.3 69.2 %all-gather.10.cloned.1.call-done = bf16[6,896,224]{2,0,1:T(8,128)(2,1)} async-done(((bf16[6,112,224]{2,0,1:T(8,128)(2,1)}), bf16[6,896,224]{2,0,1:T(8,128)(2,1)}) %all-gather.10.cloned.1.call-update) | async-done | bytes 2408464 | tf_op jit(solution)/shard_map/all_gather | solution.py:38
  78.5 6.1 %copy.67 = bf16[6,896,224]{1,2,0:T(8,128)(2,1)} copy(bf16[6,896,224]{2,0,1:T(8,128)(2,1)} %all-gather.10.cloned.1.call-done) | data formatting | bytes 4816896 | tf_op jit(solution)/shard_map/all_gather | solution.py:38
  85.6 34.5 %all_gather.27 = bf16[2,224,896]{1,0,2:T(2,128)(2,1)S(1)} all-gather(bf16[2,224,112]{1,0,2:T(2,128)(2,1)S(1)} %copy.76), channel_id=1, replica_groups=mesh['cx'=4,'cy'=2,'tp'=4] {'cx','cy'}, dimensions={2}, use_global_device_ids=true | all-gather | bytes 903168 | tf_op jit(solution)/shard_map/all_gather | solution.py:39
  123.7 7.4 %all-gather.8.cloned.1.call-done = bf16[1024,896]{1,0:T(8,128)(2,1)} async-done(((bf16[128,896]{1,0:T(8,128)(2,1)}), bf16[1024,896]{1,0:T(8,128)(2,1)}) %all-gather.8.cloned.1.call-update) | async-done | bytes 1835024 | tf_op jit(solution)/shard_map/all_gather | solution.py:37
  131.1 4.3 %gather_fusion = bf16[512,896]{1,0:T(8,128)(2,1)S(1)} fusion(bf16[1024,896]{1,0:T(8,128)(2,1)} %all-gather.8.cloned.1.call-done, s32[1024]{0:T(1024)S(1)} %pad_clamp_fusion), kind=kCustom, calls=%fused_computation | custom fusion | bytes 1837056 | tf_op jit(solution)/shard_map/jit(_take)/gather | solution.py:48
  136.2 61.5 %all-gather.12.cloned.1.call-done = bf16[6,896,896]{1,2,0:T(8,128)(2,1)} async-done(((bf16[6,896,224]{1,2,0:T(8,128)(2,1)}), bf16[6,896,896]{1,2,0:T(8,128)(2,1)}) %all-gather.12.cloned.1.call-update) | async-done | bytes 9633808 | tf_op jit(solution)/shard_map/all_gather | solution.py:51
  197.7 3.8 fusion.46
  201.5 2.9 reshape.106
  204.4 3.9 fusion.47
  208.3 4.0 reshape.107
  212.3 3.0 fusion.29
  215.3 2.7 fusion.82
  218.0 3.8 fusion.45
  221.7 3.1 reshape.105
  224.8 2.8 fusion.52
  228.4 2.8 fusion.83
  232.4 2.8 fusion.48
  239.0 2.7 fusion.56
  249.3 2.8 fusion.85
  253.7 21.0 %all-gather.18.cloned.1.call-done = bf16[896,896]{1,0:T(8,128)(2,1)} async-done(((bf16[112,896]{1,0:T(8,128)(2,1)}), bf16[896,896]{1,0:T(8,128)(2,1)}) %all-gather.18.cloned.1.call-update) | async-done | bytes 1605648 | tf_op jit(solution)/shard_map/all_gather | solution.py:40
  274.7 45.0 %all-gather.20.cloned.1.call-done = bf16[896,896]{0,1:T(8,128)(2,1)} async-done(((bf16[896,112]{0,1:T(8,128)(2,1)}), bf16[896,896]{0,1:T(8,128)(2,1)}) %all-gather.20.cloned.1.call-update) | async-done | bytes 1605648 | tf_op jit(solution)/shard_map/all_gather | solution.py:41
  319.7 31.4 %all-gather.16.cloned.1.call-done = bf16[2048,896]{1,0:T(8,128)(2,1)} async-done(((bf16[512,896]{1,0:T(8,128)(2,1)}), bf16[2048,896]{1,0:T(8,128)(2,1)}) %all-gather.16.cloned.1.call-update) | async-done | bytes 3670032 | tf_op jit(solution)/shard_map/all_gather | solution.py:66
  351.1 12.6 %fusion.16 = bf16[2048,896]{1,0:T(8,128)(2,1)} fusion(bf16[896,896]{0,1:T(8,128)(2,1)} %all-gather.20.cloned.1.call-done, bf16[2048,896]{1,0:T(8,128)(2,1)} %all-gather.16.cloned.1.call-done, bf16[896,896]{1,0:T(8,128)(2,1)} %all-gather.18.cloned.1.call-done), kind=kOutput, calls=%fused_computation.19 | convolution fusion | flops 6595018752 | bytes 10551296 | tf_op jit(solution)/shard_map/dot_general | solution.py:70
  363.7 41.4 %reduce-scatter.2.cloned.1.call-done = bf16[512,896]{1,0:T(8,128)(2,1)} async-done(((bf16[2048,896]{1,0:T(8,128)(2,1)}), bf16[512,896]{1,0:T(8,128)(2,1)}) %reduce-scatter.2.cloned.1.call-update) | async-done | bytes 917520 | tf_op jit(solution)/shard_map/reduce_scatter | solution.py:69
  (62 shorter events, 25.3 us)
Async XLA Ops:
  6.5 230.0 %copy-start = (bf16[2,64,896]{2,1,0:T(8,128)(2,1)S(1)}, bf16[2,64,896]{2,1,0:T(8,128)(2,1)}, u32[]{:S(2)}) copy-start(bf16[2,64,896]{2,1,0:T(8,128)(2,1)} %param.9) | copy-start | bytes 688132
  6.5 71.9 %all-gather.10.cloned.1.call-start = ((), (), s32[]{:S(2)}) async-start(), calls=%async_computation.2 | async-start | bytes 4128768 | tf_op jit(solution)/shard_map/all_gather | solution.py:38
  8.5 122.6 %all-gather.8.cloned.1.call-start = ((), (), s32[]{:S(2)}) async-start(), calls=%async_computation.1 | async-start | bytes 2064384 | tf_op jit(solution)/shard_map/all_gather | solution.py:37
  9.2 188.5 %all-gather.12.cloned.1.call-start = ((), (), s32[]{:S(2)}) async-start(), calls=%async_computation.3 | async-start | bytes 12042240 | tf_op jit(solution)/shard_map/all_gather | solution.py:51
  84.6 0.9 copy-start.5
  84.6 143.8 %all-gather.14.cloned.1.call-start = ((), (), s32[]{:S(2)}) async-start(), calls=%async_computation.4 | async-start | bytes 4014080 | tf_op jit(solution)/shard_map/all_gather | solution.py:52
  85.6 38.0 %copy-start.6 = (s32[2,2,128]{2,1,0:T(2,128)S(1)}, s32[2,2,128]{2,1,0:T(2,128)}, u32[]{:S(2)}) copy-start(s32[2,2,128]{2,1,0:T(2,128)} %param.8) | copy-start | bytes 6148
  85.6 38.0 %copy-start.7 = (f32[3,896]{1,0:T(4,128)S(1)}, f32[3,896]{1,0:T(4,128)}, u32[]{:S(2)}) copy-start(f32[3,896]{1,0:T(4,128)} %param.13) | copy-start | bytes 32260
  122.4 152.3 %all-gather.18.cloned.1.call-start = ((), (), s32[]{:S(2)}) async-start(), calls=%async_computation.6 | async-start | bytes 1806336 | tf_op jit(solution)/shard_map/all_gather | solution.py:40
  122.9 196.7 %all-gather.20.cloned.1.call-start = ((), (), s32[]{:S(2)}) async-start(), calls=%async_computation.7 | async-start | bytes 1806336 | tf_op jit(solution)/shard_map/all_gather | solution.py:41
  123.5 227.6 %all-gather.16.cloned.1.call-start = ((), (), s32[]{:S(2)}) async-start(), calls=%async_computation.5 | async-start | bytes 4587520 | tf_op jit(solution)/shard_map/all_gather | solution.py:66
  231.2 1.2 copy-start.2
  243.8 1.3 copy-start.4
  247.8 1.5 copy-start.3
  253.7 151.4 %reduce-scatter.2.cloned.1.call-start = ((), (), s32[]{:S(2)}) async-start(), calls=%async_computation.8 | async-start | bytes 4587520 | tf_op jit(solution)/shard_map/reduce_scatter | solution.py:69
  363.7 43.6 %copy-start.1 = (bf16[2,64,896]{2,1,0:T(8,128)(2,1)S(1)}, bf16[2,64,896]{2,1,0:T(8,128)(2,1)}, u32[]{:S(2)}) copy-start(bf16[2,64,896]{2,1,0:T(8,128)(2,1)} %param.9) | copy-start | bytes 688132
Sparse Core Ops, SparseCore 0:
  9.5 68.9 all-gather.9
  80.7 50.3 all-gather.7
  132.6 65.0 all-gather.11
  199.1 28.8 all-gather.13
  230.1 44.5 all-gather.17
  276.7 42.9 all-gather.19
  321.2 29.8 all-gather.15
  363.8 41.2 reduce-scatter.1
where the time goes:
time: 415 us; the launch traced here: 414 us
  waiting for transfers between devices  279 us (67%)
  matrix products  45.8 us (11%)
  blocking collectives  34.5 us (8%)
  local copies, waits for them, and re-layouts  32.9 us (8%)
  between operations  13.7 us (3%)
  other arithmetic  8.18 us (2%)
    all_gather x1, waiting for transfers between devices, body(): lax.all_gather(attn_in, ('cx', 'cy'), axis=1, tiled=True)  69.2 us
    all_gather x1, waiting for transfers between devices, body(): lax.all_gather(in_w, 'tp', axis=2, tiled=True)  61.5 us
    all_gather x1, waiting for transfers between devices, body(): lax.all_gather(w_down, ('cx', 'cy'), axis=1, tiled=True)  45 us
    reduce_scatter x1, waiting for transfers between devices, body(): lax.psum_scatter(jnp.dot(act, down_w, preferred_element_type=jnp.float32)...  41.4 us
    all_gather x1, blocking collectives, body(): lax.all_gather(attn_out, ('cx', 'cy'), axis=2, tiled=True)  34.5 us
    all_gather x1, waiting for transfers between devices, body(): every = lax.all_gather(h_three, 'tp', axis=0, tiled=True)  31.4 us
    all_gather x1, waiting for transfers between devices, body(): lax.all_gather(w_up, ('cx', 'cy'), axis=0, tiled=True)  21 us
    dot_general x6, matrix products, project(): jnp.dot(hidden, matrix, preferred_element_type=jnp.float32)  18.9 us
  transfers between devices with their start and end apart: 8, of which 7 were waited for; matrix products, arithmetic and copies ran while one was open for 16% of the time, Pallas kernels for 0%

commit v1 on v0

--- a/solution.py
+++ b/solution.py
@@ -63,7 +63,12 @@
     cross = attend(cross_q, cross_k, cross_v).reshape(total, width)
     x_two = x_one + jnp.dot(cross, out_full[1], preferred_element_type=jnp.float32)
     h_three = layer_norm(x_two, gains[2])
-    every = lax.all_gather(h_three, "tp", axis=0, tiled=True)
+    ring = [h_three]
+    for hop in range(3):
+        ring.append(lax.ppermute(ring[-1], "tp", [(dev, (dev + 1) % 4) for dev in range(4)]))
+    every = jnp.roll(
+        jnp.concatenate(ring[::-1], axis=0), (lax.axis_index("tp") + 1) * ring[0].shape[0], axis=0
+    )
     upward = jnp.dot(every, up_w, preferred_element_type=jnp.float32)
     act = jax.nn.gelu(upward, approximate=True).astype(jnp.bfloat16)
     mixed = lax.psum_scatter(

time: 415 us -> 383 us (0.923)
  waiting for transfers between devices: 279 us -> 235 us
  local copies, waits for them, and re-layouts: 32.9 us -> 43 us
    ppermute x0 -> x3, waiting for transfers between devices: none -> 38.6 us  [body(): lax.ppermute(ring[-1], 'tp', [(dev, (dev + 1) % 4) for dev in range(4)])]
    all_gather x1 -> x0, waiting for transfers between devices: 31.4 us -> none  [body(): every = lax.all_gather(h_three, 'tp', axis=0, tiled=True)]
    all_gather x1, waiting for transfers between devices: 45 us -> 16.1 us  [body(): lax.all_gather(w_down, ('cx', 'cy'), axis=1, tiled=True)]
    all_gather x1, waiting for transfers between devices: 21 us -> 0.01 us  [body(): lax.all_gather(w_up, ('cx', 'cy'), axis=0, tiled=True)]
    unnamed x19 -> x25, local copies, waits for them, and re-layouts: 5.52 us -> 16.5 us
  transfers between devices with their start and end apart: 8 -> 10, of which waited for: 7 -> 8; matrix products, arithmetic and copies ran while one was open for 16% -> 20% of each run, Pallas kernels for 0% -> 0%
where the time goes in v1:
time: 383 us; the launch traced here: 382 us
  waiting for transfers between devices  235 us (61%)
  matrix products  45.1 us (12%)
  local copies, waits for them, and re-layouts  43 us (11%)
  blocking collectives  34.4 us (9%)
  between operations  13.8 us (4%)
  other arithmetic  9.73 us (3%)
    all_gather x1, waiting for transfers between devices, body(): lax.all_gather(attn_in, ('cx', 'cy'), axis=1, tiled=True)  69.2 us
    all_gather x1, waiting for transfers between devices, body(): lax.all_gather(in_w, 'tp', axis=2, tiled=True)  62 us
    reduce_scatter x1, waiting for transfers between devices, body(): lax.psum_scatter(jnp.dot(act, down_w, preferred_element_type=jnp.float32)...  39.7 us
    ppermute x3, waiting for transfers between devices, body(): lax.ppermute(ring[-1], 'tp', [(dev, (dev + 1) % 4) for dev in range(4)])  38.6 us
    all_gather x1, blocking collectives, body(): lax.all_gather(attn_out, ('cx', 'cy'), axis=2, tiled=True)  34.4 us
    dot_general x6, matrix products, project(): jnp.dot(hidden, matrix, preferred_element_type=jnp.float32)  18.2 us
    unnamed x25, local copies, waits for them, and re-layouts  16.5 us
    all_gather x1, waiting for transfers between devices, body(): lax.all_gather(w_down, ('cx', 'cy'), axis=1, tiled=True)  16.1 us
  transfers between devices with their start and end apart: 10, of which 8 were waited for; matrix products, arithmetic and copies ran while one was open for 20% of the time, Pallas kernels for 0%

profile of v1, /device:TPU:0, one launch (start us, length us, event | category | flops | bytes accessed | tf_op | source)
XLA Modules:
  0.0 381.5 jit_solution(16135998232159568422)
XLA Ops:
  9.3 69.2 %all-gather.9.cloned.1.call-done = bf16[6,896,224]{2,0,1:T(8,128)(2,1)} async-done(((bf16[6,112,224]{2,0,1:T(8,128)(2,1)}), bf16[6,896,224]{2,0,1:T(8,128)(2,1)}) %all-gather.9.cloned.1.call-update) | async-done | bytes 2408464 | tf_op jit(solution)/shard_map/all_gather | solution.py:38
  78.5 6.1 %copy.67 = bf16[6,896,224]{1,2,0:T(8,128)(2,1)} copy(bf16[6,896,224]{2,0,1:T(8,128)(2,1)} %all-gather.9.cloned.1.call-done) | data formatting | bytes 4816896 | tf_op jit(solution)/shard_map/all_gather | solution.py:38
  85.7 34.4 %all_gather.24 = bf16[2,224,896]{1,0,2:T(2,128)(2,1)S(1)} all-gather(bf16[2,224,112]{1,0,2:T(2,128)(2,1)S(1)} %copy.76), channel_id=1, replica_groups=mesh['cx'=4,'cy'=2,'tp'=4] {'cx','cy'}, dimensions={2}, use_global_device_ids=true | all-gather | bytes 903168 | tf_op jit(solution)/shard_map/all_gather | solution.py:39
  123.1 8.0 %all-gather.7.cloned.1.call-done = bf16[1024,896]{1,0:T(8,128)(2,1)} async-done(((bf16[128,896]{1,0:T(8,128)(2,1)}), bf16[1024,896]{1,0:T(8,128)(2,1)}) %all-gather.7.cloned.1.call-update) | async-done | bytes 1835024 | tf_op jit(solution)/shard_map/all_gather | solution.py:37
  131.1 4.3 %gather_fusion = bf16[512,896]{1,0:T(8,128)(2,1)S(1)} fusion(bf16[1024,896]{1,0:T(8,128)(2,1)} %all-gather.7.cloned.1.call-done, s32[1024]{0:T(1024)S(1)} %pad_clamp_fusion), kind=kCustom, calls=%fused_computation | custom fusion | bytes 1837056 | tf_op jit(solution)/shard_map/jit(_take)/gather | solution.py:48
  136.2 62.0 %all-gather.11.cloned.1.call-done = bf16[6,896,896]{1,2,0:T(8,128)(2,1)} async-done(((bf16[6,896,224]{1,2,0:T(8,128)(2,1)}), bf16[6,896,896]{1,2,0:T(8,128)(2,1)}) %all-gather.11.cloned.1.call-update) | async-done | bytes 9633808 | tf_op jit(solution)/shard_map/all_gather | solution.py:51
  198.2 3.8 fusion.52
  202.0 2.9 reshape.106
  204.9 3.9 %fusion.53 = bf16[512,896]{1,0:T(8,128)(2,1)} fusion(bf16[6,896,896]{1,2,0:T(8,128)(2,1)} %all-gather.11.cloned.1.call-done, f32[896]{0:T(1024)S(1)} %get-tuple-element.6, f32[512]{0:T(512)S(1)} %add_rsqrt_fusion.2, f32[512]{0:T(512)S(1)} %broadcast_multiply_fusion.2, bf16[512,896]{1,0:T(8,128)(2,1)S(1)} %gather_fusion, pred[512]{0:T(512)(128)(4,1)S(1)} %compare_and_fusion), kind=kOutput, calls=%fused_computation.68 | convolution fusion | flops 825294848 | bytes 3448832 | tf_op jit(solution)/shard_map/dot_general | solution.py:17
  208.8 4.0 %reshape.107 = bf16[4,128,14,64]{3,2,1,0:T(8,128)(2,1)} reshape(bf16[512,896]{1,0:T(8,128)(2,1)} %fusion.53) | data formatting | bytes 1835008 | tf_op jit(solution)/shard_map/reshape;reshape | solution.py:25
  212.8 3.0 fusion.31
  215.8 2.7 fusion.90
  218.5 3.8 fusion.51
  222.2 3.1 reshape.105
  225.3 2.8 fusion.58
  228.9 2.8 fusion.91
  232.9 2.8 fusion.54
  248.2 2.8 fusion.93
  251.9 12.6 %collective-permute-done = bf16[512,896]{1,0:T(8,128)(2,1)S(1)} collective-permute-done((bf16[512,896]{1,0:T(8,128)(2,1)S(1)}, bf16[512,896]{1,0:T(8,128)(2,1)S(1)}, u32[]{:S(2)}, u32[]{:S(2)}) %collective-permute-start) | collective-permute-done | bytes 917536 | tf_op jit(solution)/shard_map/ppermute | solution.py:68
  264.6 12.8 %collective-permute-done.1 = bf16[512,896]{1,0:T(8,128)(2,1)} collective-permute-done((bf16[512,896]{1,0:T(8,128)(2,1)S(1)}, bf16[512,896]{1,0:T(8,128)(2,1)}, u32[]{:S(2)}, u32[]{:S(2)}) %collective-permute-start.1) | collective-permute-done | bytes 917536 | tf_op jit(solution)/shard_map/ppermute | solution.py:68
  277.5 13.1 %collective-permute-done.2 = bf16[512,896]{1,0:T(8,128)(2,1)} collective-permute-done((bf16[512,896]{1,0:T(8,128)(2,1)}, bf16[512,896]{1,0:T(8,128)(2,1)}, u32[]{:S(2)}, u32[]{:S(2)}) %collective-permute-start.2) | collective-permute-done | bytes 917536 | tf_op jit(solution)/shard_map/ppermute | solution.py:68
  303.9 16.1 %all-gather.17.cloned.1.call-done = bf16[896,896]{0,1:T(8,128)(2,1)} async-done(((bf16[896,112]{0,1:T(8,128)(2,1)}), bf16[896,896]{0,1:T(8,128)(2,1)}) %all-gather.17.cloned.1.call-update) | async-done | bytes 1605648 | tf_op jit(solution)/shard_map/all_gather | solution.py:41
  320.1 12.6 %fusion.18 = bf16[2048,896]{1,0:T(8,128)(2,1)} fusion(bf16[896,896]{0,1:T(8,128)(2,1)} %all-gather.17.cloned.1.call-done, bf16[896,896]{1,0:T(8,128)(2,1)} %all-gather.15.cloned.1.call-done, bf16[4096,896]{1,0:T(8,128)(2,1)} %constant_dynamic-update-slice_fusion, s32[]{:T(128)S(6)} %select_n.37), kind=kOutput, calls=%fused_computation.21 | convolution fusion | flops 6595018752 | bytes 10551300 | tf_op jit(solution)/shard_map/dot_general | solution.py:75
  332.7 39.7 %reduce-scatter.2.cloned.1.call-done = bf16[512,896]{1,0:T(8,128)(2,1)} async-done(((bf16[2048,896]{1,0:T(8,128)(2,1)}), bf16[512,896]{1,0:T(8,128)(2,1)}) %reduce-scatter.2.cloned.1.call-update) | async-done | bytes 917520 | tf_op jit(solution)/shard_map/reduce_scatter | solution.py:74
  (73 shorter events, 38.5 us)
Async XLA Ops:
  6.5 230.6 %copy-start = (bf16[2,64,896]{2,1,0:T(8,128)(2,1)S(1)}, bf16[2,64,896]{2,1,0:T(8,128)(2,1)}, u32[]{:S(2)}) copy-start(bf16[2,64,896]{2,1,0:T(8,128)(2,1)} %param.9) | copy-start | bytes 688132
  6.5 71.9 %all-gather.9.cloned.1.call-start = ((), (), s32[]{:S(2)}) async-start(), calls=%async_computation.2 | async-start | bytes 4128768 | tf_op jit(solution)/shard_map/all_gather | solution.py:38
  8.5 122.6 %all-gather.7.cloned.1.call-start = ((), (), s32[]{:S(2)}) async-start(), calls=%async_computation.1 | async-start | bytes 2064384 | tf_op jit(solution)/shard_map/all_gather | solution.py:37
  9.2 189.0 %all-gather.11.cloned.1.call-start = ((), (), s32[]{:S(2)}) async-start(), calls=%async_computation.3 | async-start | bytes 12042240 | tf_op jit(solution)/shard_map/all_gather | solution.py:51
  84.6 0.9 copy-start.5
  84.6 144.3 %all-gather.13.cloned.1.call-start = ((), (), s32[]{:S(2)}) async-start(), calls=%async_computation.4 | async-start | bytes 4014080 | tf_op jit(solution)/shard_map/all_gather | solution.py:52
  85.6 37.4 %copy-start.6 = (s32[2,2,128]{2,1,0:T(2,128)S(1)}, s32[2,2,128]{2,1,0:T(2,128)}, u32[]{:S(2)}) copy-start(s32[2,2,128]{2,1,0:T(2,128)} %param.8) | copy-start | bytes 6148
  85.6 37.4 %copy-start.7 = (f32[3,896]{1,0:T(4,128)S(1)}, f32[3,896]{1,0:T(4,128)}, u32[]{:S(2)}) copy-start(f32[3,896]{1,0:T(4,128)} %param.13) | copy-start | bytes 32260
  122.3 181.6 %all-gather.15.cloned.1.call-start = ((), (), s32[]{:S(2)}) async-start(), calls=%async_computation.5 | async-start | bytes 1806336 | tf_op jit(solution)/shard_map/all_gather | solution.py:40
  122.9 197.1 %all-gather.17.cloned.1.call-start = ((), (), s32[]{:S(2)}) async-start(), calls=%async_computation.6 | async-start | bytes 1806336 | tf_op jit(solution)/shard_map/all_gather | solution.py:41
  231.7 1.3 copy-start.2
  240.3 1.2 copy-start.4
  246.7 1.5 copy-start.3
  251.7 12.9 %collective-permute-start = (bf16[512,896]{1,0:T(8,128)(2,1)S(1)}, bf16[512,896]{1,0:T(8,128)(2,1)S(1)}, u32[]{:S(2)}, u32[]{:S(2)}) collective-permute-start(bf16[512,896]{1,0:T(8,128)(2,1)S(1)} %multiply_convert_fusion), channel_id=1, source_target_pairs={{0,1},{1,2},{2,3},{3,0},{4,5},{5,6},{6,7},{7,4},{8,9},{9,10},{10,1... | collective-permute-start | bytes 2752520 | tf_op jit(solution)/shard_map/ppermute | solution.py:68
  264.5 12.9 %collective-permute-start.1 = (bf16[512,896]{1,0:T(8,128)(2,1)S(1)}, bf16[512,896]{1,0:T(8,128)(2,1)}, u32[]{:S(2)}, u32[]{:S(2)}) collective-permute-start(bf16[512,896]{1,0:T(8,128)(2,1)S(1)} %collective-permute-done), channel_id=1, source_target_pairs={{0,1},{1,2},{2,3},{3,0},{4,5},{5,6},{6,7},{7,4},{8,9},{9,10},{10,1... | collective-permute-start | bytes 2752520 | tf_op jit(solution)/shard_map/ppermute | solution.py:68
  264.6 107.9 %reduce-scatter.2.cloned.1.call-start = ((), (), s32[]{:S(2)}) async-start(), calls=%async_computation.7 | async-start | bytes 4587520 | tf_op jit(solution)/shard_map/reduce_scatter | solution.py:74
  277.4 13.1 %collective-permute-start.2 = (bf16[512,896]{1,0:T(8,128)(2,1)}, bf16[512,896]{1,0:T(8,128)(2,1)}, u32[]{:S(2)}, u32[]{:S(2)}) collective-permute-start(bf16[512,896]{1,0:T(8,128)(2,1)} %collective-permute-done.1), channel_id=1, source_target_pairs={{0,1},{1,2},{2,3},{3,0},{4,5},{5,6},{6,7},{7,4},{8,9},{9,10},{10,1... | collective-permute-start | bytes 2752520 | tf_op jit(solution)/shard_map/ppermute | solution.py:68
  332.7 42.0 %copy-start.1 = (bf16[2,64,896]{2,1,0:T(8,128)(2,1)S(1)}, bf16[2,64,896]{2,1,0:T(8,128)(2,1)}, u32[]{:S(2)}) copy-start(bf16[2,64,896]{2,1,0:T(8,128)(2,1)} %param.9) | copy-start | bytes 688132
Sparse Core Ops, SparseCore 0:
  9.5 68.9 all-gather.8
  80.7 50.3 all-gather.6
  132.7 65.5 all-gather.10
  199.6 28.8 all-gather.12
  230.6 44.5 all-gather.14
  277.2 42.8 all-gather.16
  332.8 39.5 reduce-scatter.1
